TPU v7x, 256 devices: a whole 4x4x8 slice. The times are simulated.
256 devices in a mesh: branch: 32 (over y, z), tensor: 8 (over x, core).
Axes of the slice: x: 4, y: 4, z: 8, core: 2. Of those that a mesh axis runs over, the one named last changes fastest.
Arguments:
- layer_input: bfloat16 [16384, 5120], P(('branch', 'tensor')), may hold values from -360 to 360
- norm_gain: float32 [5120], replicated, may hold values from 0.25 to 1.75
- projection_weight: bfloat16 [5120, 5120], P(None, 'tensor'), may hold values from -0.078125 to 0.078125
- output_weight: bfloat16 [3072, 5120], P('tensor'), may hold values from -3 to 3
- prompt_cache: bfloat16 [2048, 2048], P(None, 'tensor'), may hold values from -1800 to 1800
- subtree_cache: bfloat16 [2, 16384, 2048], P(None, 'branch', 'tensor'), may hold values from -6 to 6
- parents: int32 [2, 32], replicated, may hold values from 0 to 31
- leaf_scores: float32 [32], P('branch'), may hold values from 0.3 to 1
Outputs:
- attn_output: bfloat16 [16384, 5120], P(('branch', 'tensor'))
- subtree_min: float32 [2, 32], P(None, 'branch')
- subtree_product: float32 [2, 32], P(None, 'branch')
Inputs may be any that keep to these rules, and one draw needn't show every extreme that they name: parents[0, j] is the parent in level one of node j of level two; parents[1, j] is the parent in level two of new node j. Node j of every level is held by branch index j.
All inputs are finite; a program needn't handle non-finite values.
Results may differ from a plain program's by a relative error of at most 0.015.
Values may be sent and summed in bfloat16 or wider, within the bound.
No kernel may reach another device: no remote copies, remote signals or barrier semaphores. Data moves between devices by JAX's collectives and lax.ppermute only.
A program may use at most 128 MiB of HBM per device.

v0:
```python
import jax
import jax.numpy as jnp
from jax import lax
from jax.sharding import PartitionSpec as P

HEAD_SIZE = 128
SEGMENT_TOKENS = 512
PROMPT_TOKENS = 2048
THETA = 1000000.0
EPSILON = 1e-06


def from_everyone(x, axis):
    count = lax.axis_size(axis)
    return lax.all_to_all(jnp.broadcast_to(x[None], (count, *x.shape)), axis, 0, 0, tiled=True)


def all_in_one(x, axis):
    leaves = jax.tree.leaves(x)
    sequence = sorted(range(len(leaves)), key=lambda k: -leaves[k].size)
    width = (1, *leaves[sequence[0]].shape)[-1]
    lines = [
        jnp.pad(leaves[k].reshape(-1), (0, -leaves[k].size % width)).reshape(-1, width)
        for k in sequence
    ]
    both, at, found = (from_everyone(jnp.concatenate(lines), axis), 0, {})
    for k, line in zip(sequence, lines):
        piece = both[:, at : at + len(line)].reshape(len(both), -1)
        found[k] = piece[:, : leaves[k].size].reshape(-1, *leaves[k].shape)
        at += len(line)
    numbers = iter(range(len(leaves)))
    return jax.tree.map(lambda _: found[next(numbers)], x)


def combined_pairwise(pieces, combine):
    while len(jax.tree.leaves(pieces)[0]) > 1:
        pieces = jax.vmap(combine)(
            *(jax.tree.map(lambda part: part[side::2], pieces) for side in (0, 1))
        )
    return jax.tree.map(lambda part: part[0], pieces)


def combined_all(x, axis, combine):
    pieces = all_in_one(x, axis)
    return combined_pairwise(pieces, combine)


def normalize(inputs, gain):
    wide = inputs.astype(jnp.float32)
    scale = lax.rsqrt(jnp.mean(wide * wide, axis=-1, keepdims=True) + EPSILON)
    return (wide * scale * gain).astype(jnp.bfloat16)


def rotate(vectors, offset):
    half = vectors.shape[-1] // 2
    freq = THETA ** (-jnp.arange(half, dtype=jnp.float32) * 2.0 / vectors.shape[-1])
    places = (offset + jnp.arange(vectors.shape[0])).astype(jnp.float32)
    angle = places[:, None] * freq[None, :]
    shape = (vectors.shape[0],) + (1,) * (vectors.ndim - 2) + (half,)
    cosine = jnp.cos(angle).reshape(shape)
    sine = jnp.sin(angle).reshape(shape)
    front = vectors[..., :half]
    back = vectors[..., half:]
    return jnp.concatenate([front * cosine - back * sine, back * cosine + front * sine], -1)


def attend(queries, context):
    keys = context[:, :, 0, :]
    values = context[:, :, 1, :]
    scale = queries.shape[-1] ** (-0.5)
    scores = jnp.einsum("skgd,lkd->kgsl", queries, keys, preferred_element_type=jnp.float32) * scale
    total = context.shape[0]
    count = queries.shape[0]
    key_place = jnp.arange(total)
    query_place = jnp.arange(count) + total - count
    visible = key_place[None, :] <= query_place[:, None]
    scores = jnp.where(visible, scores, -jnp.inf)
    top = jnp.max(scores, axis=-1, keepdims=True)
    expos = jnp.exp(scores - top)
    weights = (expos / jnp.sum(expos, axis=-1, keepdims=True)).astype(jnp.bfloat16)
    mixed = jnp.einsum("kgsl,lkd->skgd", weights, values, preferred_element_type=jnp.float32)
    return mixed.astype(jnp.bfloat16).reshape(count, -1)


def pair_combine(left, right):
    return (jnp.minimum(left[0], right[0]), left[1] * right[1])


def per_device(
    layer_input,
    norm_gain,
    projection_weight,
    output_weight,
    prompt_cache,
    subtree_cache,
    parents,
    leaf_scores,
):
    kv_heads = prompt_cache.shape[1] // (2 * HEAD_SIZE)
    group = projection_weight.shape[1] // (kv_heads * HEAD_SIZE) - 2
    offset = PROMPT_TOKENS + 2 * SEGMENT_TOKENS
    normed = normalize(layer_input, norm_gain)
    packed = jnp.dot(
        lax.all_gather(normed, "tensor", axis=0, tiled=True),
        projection_weight,
        preferred_element_type=jnp.float32,
    )
    packed = packed.reshape(SEGMENT_TOKENS, kv_heads, group + 2, HEAD_SIZE)
    queries = rotate(packed[:, :, :group, :], offset).astype(jnp.bfloat16)
    keys = rotate(packed[:, :, group, :], offset).astype(jnp.bfloat16)
    values = packed[:, :, group + 1, :].astype(jnp.bfloat16)
    own = jnp.stack([keys, values], 2)
    second = parents[1]
    first = parents[0][second]
    position = lax.axis_index("branch")
    held = lax.all_to_all(subtree_cache[None], "branch", split_axis=2, concat_axis=0, tiled=True)
    tree_levels = jnp.arange(2, dtype=jnp.int32)
    picks = jnp.stack([first, second], 1)
    outgoing = held[picks, tree_levels[None, :]]
    arrived = lax.all_to_all(outgoing, "branch", split_axis=0, concat_axis=2, tiled=True)
    blocks = arrived[0]
    blocks = blocks.reshape(2 * SEGMENT_TOKENS, kv_heads, 2, HEAD_SIZE)
    prompt = prompt_cache.reshape(-1, kv_heads, 2, HEAD_SIZE)
    context = jnp.concatenate([prompt, blocks, own], 0)
    mixed = attend(queries, context)
    partial_term = jnp.dot(mixed, output_weight, preferred_element_type=jnp.float32)
    summed = lax.psum_scatter(
        partial_term.astype(jnp.bfloat16).astype(jnp.float32).astype(jnp.bfloat16),
        "tensor",
        scatter_dimension=0,
        tiled=True,
    )
    nodes = jnp.arange(parents.shape[1], dtype=jnp.int32)
    marks = jnp.stack([nodes == first[position], nodes == second[position]], 0)
    filled = jnp.where(marks, leaf_scores[0], 1.0)
    lowest, product = combined_all((filled, filled), "branch", pair_combine)
    subtree_min = lax.dynamic_slice_in_dim(lowest, position, 1, 1)
    subtree_product = lax.dynamic_slice_in_dim(product, position, 1, 1)
    return (summed, subtree_min, subtree_product)


def solution(mesh):
    placed = (
        P(("branch", "tensor"), None),
        P(),
        P(None, "tensor"),
        P("tensor", None),
        P(None, "tensor"),
        P(None, "branch", "tensor"),
        P(),
        P("branch"),
    )
    return jax.shard_map(
        per_device,
        mesh=mesh,
        in_specs=placed,
        out_specs=(P(("branch", "tensor"), None), P(None, "branch"), P(None, "branch")),
        check_vma=False,
    )
```

profile of v0, /device:TPU:8, one launch (start us, length us, event | category | flops | bytes accessed | tf_op | source)
XLA Modules:
  0.0 169.4 jit_solution(4992892851186095734)
XLA Ops:
  7.2 1.3 fusion.4
  8.5 2.2 %fusion.6 = bf16[64,5120]{1,0:T(8,128)(2,1)} fusion(bf16[64,5120]{1,0:T(8,128)(2,1)} %param.8, f32[5120]{0:T(1024)} %param.9, f32[64]{0:T(128)S(1)} %add_rsqrt_fusion), kind=kLoop, calls=%fused_computation.16 | loop fusion | flops 1310720 | bytes 1331456 | tf_op jit(solution)/shard_map/convert_element_type | solution.py:51
  10.7 2.4 %copy.95 = bf16[2,512,256]{2,0,1:T(2,128)(2,1)} copy(bf16[2,512,256]{2,1,0:T(8,128)(2,1)} %param.13) | data formatting | bytes 1048576 | tf_op args[5]
  13.1 11.7 %all-to-all-start = ((bf16[1,2,512,256]{3,1,0,2:T(2,128)(2,1)}), bf16[1,2,512,256]{3,1,0,2:T(2,128)(2,1)S(1)}, u32[]{:S(2)}, u32[]{:S(2)}) async-start(bf16[1,2,512,256]{3,1,0,2:T(2,128)(2,1)} %bitcast.82), calls=%async_computation | async-start | bytes 1048576 | tf_op jit(solution)/shard_map/all_to_all | solution.py:116
  24.8 0.7 fusion.30
  25.5 0.8 fusion.36
  26.3 0.7 gather_fusion
  27.2 1.5 copy.67
  29.4 1.8 %multiply_cosine_fusion = (f32[512,64]{1,0:T(8,128)}, f32[512,64]{1,0:T(8,128)}) fusion(f32[64]{0:T(128)S(1)} %multiply_power_fusion, f32[512]{0:T(512)S(1)} %fusion.29), kind=kLoop, calls=%fused_computation.31 | loop fusion | flops 32768 | bytes 264448 | tf_op jit(solution)/shard_map/cos | solution.py:60
  31.2 9.0 %all-to-all-done = bf16[1,2,512,256]{3,1,0,2:T(2,128)(2,1)S(1)} async-done(((bf16[1,2,512,256]{3,1,0,2:T(2,128)(2,1)}), bf16[1,2,512,256]{3,1,0,2:T(2,128)(2,1)S(1)}, u32[]{:S(2)}, u32[]{:S(2)}) %all-to-all-start) | async-done | bytes 524320 | tf_op jit(solution)/shard_map/all_to_all | solution.py:116
  40.4 1.5 gather_fusion.1
  41.9 7.0 %all-to-all-start.1 = ((bf16[32,2,16,256]{3,2,1,0:T(8,128)(2,1)}), bf16[32,2,16,256]{3,2,1,0:T(8,128)(2,1)S(1)}, u32[]{:S(2)}, u32[]{:S(2)}) async-start(bf16[32,2,16,256]{3,2,1,0:T(8,128)(2,1)} %bitcast.10), calls=%async_computation.1 | async-start | bytes 1048576 | tf_op jit(solution)/shard_map/all_to_all | solution.py:120
  49.1 1.5 iota_compare_fusion
  50.6 13.0 %all-to-all-done.1 = bf16[32,2,16,256]{3,2,1,0:T(8,128)(2,1)S(1)} async-done(((bf16[32,2,16,256]{3,2,1,0:T(8,128)(2,1)}), bf16[32,2,16,256]{3,2,1,0:T(8,128)(2,1)S(1)}, u32[]{:S(2)}, u32[]{:S(2)}) %all-to-all-start.1) | async-done | bytes 524320 | tf_op jit(solution)/shard_map/all_to_all | solution.py:120
  63.7 0.8 copy.72
  64.5 1.2 reshape_squeeze.3
  65.7 0.9 copy.77
  66.6 8.4 %fusion.37 = f32[512,640]{0,1:T(8,128)S(1)} fusion(bf16[512,5120]{1,0:T(8,128)(2,1)} %all-gather.2.cloned.1.call-done, bf16[5120,640]{1,0:T(8,128)(2,1)} %param.10), kind=kOutput, calls=%fused_computation.80 | convolution fusion | flops 3355443200 | bytes 13107200 | tf_op jit(solution)/shard_map/dot_general | solution.py:103
  75.0 0.9 fusion.34
  76.2 1.9 %fusion.25 = (bf16[512,1,1,64]{3,0,2,1:T(8,128)(2,1)}, bf16[512,1,1,64]{3,0,2,1:T(8,128)(2,1)}) fusion(f32[512,1,128]{2,0,1:T(8,128)S(1)} %bitcast.85, f32[64]{0:T(128)S(1)} %multiply_power_fusion, f32[512]{0:T(512)S(1)} %fusion.29), kind=kLoop, calls=%fused_computation.43 | loop fusion | flops 294912 | bytes 395520 | tf_op jit(solution)/shard_map/concatenate | solution.py:64
  78.1 2.2 %copy.91 = f32[512,1,3,64]{3,0,2,1:T(8,128)} copy(f32[512,1,3,64]{0,3,2,1:T(8,128)} %get-tuple-element.5) | data formatting | bytes 786432
  80.3 2.2 %copy.90 = f32[512,1,3,64]{3,0,2,1:T(8,128)} copy(f32[512,1,3,64]{0,3,2,1:T(8,128)} %get-tuple-element.6) | data formatting | bytes 786432
  82.5 2.6 %fusion.11 = (bf16[512,3,64]{2,0,1:T(8,128)(2,1)}, bf16[512,3,64]{2,0,1:T(8,128)(2,1)}) fusion(f32[512,1,3,64]{3,0,2,1:T(8,128)} %copy.91, f32[512,1,3,64]{3,0,2,1:T(8,128)} %copy.90, f32[512,64]{1,0:T(8,128)} %get-tuple-element.12, f32[512,64]{1,0:T(8,128)} %get-tuple-element.11), kind=kLoop, calls=%fused_computation.25 | loop fusion | flops 786432 | bytes 1441792 | tf_op jit(solution)/shard_map/concatenate | solution.py:64
  85.1 2.4 %maximum_maximum_fusion = bf16[3584,1,2,128]{3,0,2,1:T(8,128)(2,1)} fusion(bf16[512,1,1,128]{3,0,2,1:T(8,128)(2,1)S(1)} %copy.89, bf16[512,1,1,64]{3,0,2,1:T(8,128)(2,1)} %get-tuple-element.8, bf16[512,1,1,64]{3,0,2,1:T(8,128)(2,1)} %get-tuple-element.7, bf16[1024,1,2,128]{3,0,2,1:T(8,128)(2,1)S(1)} %copy-done.2, bf16[2048,1,2,128]{3,0,2,1:T(8,128)(2,1)S(1)} %copy.76), kind=kLoop, calls=%fused_computation.11 | loop fusion | flops 9175040 | bytes 3670016 | tf_op jit(solution)/shard_map/concatenate | solution.py:124
  87.5 5.6 %fusion.1 = (f32[3,512]{1,0:T(4,128)S(1)}, f32[3584,512,3]{1,0,2:T(8,128)S(1)}) fusion(pred[512,3584]{0,1:T(8,128)(4,1)S(1)} %iota_compare_fusion, bf16[512,3,64]{2,0,1:T(8,128)(2,1)} %get-tuple-element.4, bf16[512,3,64]{2,0,1:T(8,128)(2,1)} %get-tuple-element.3, bf16[3584,1,2,128]{3,0,2,1:T(8,128)(2,1)} %maximum_maximum_fusion), kind=kOutput, calls=%fused_computation.6 | convolution fusion | flops 1426586112 | bytes 25565184 | tf_op jit(solution)/shard_map/skgd,lkd->kgsl/dot_general | solution.py:71
  93.1 7.3 %copy-done = f32[3584,512,3]{1,0,2:T(8,128)} copy-done((f32[3584,512,3]{1,0,2:T(8,128)}, f32[3584,512,3]{1,0,2:T(8,128)S(1)}, u32[]{:S(2)}) %copy-start) | copy-done | bytes 22020120
  100.4 5.0 %fusion = f32[3,512]{1,0:T(4,128)S(1)} fusion(f32[3584,512,3]{1,0,2:T(8,128)S(1)} %get-tuple-element.17, f32[3,512]{1,0:T(4,128)S(1)} %get-tuple-element.16, pred[512,3584]{0,1:T(8,128)(4,1)S(1)} %iota_compare_fusion), kind=kLoop, calls=%fused_computation.5 | loop fusion | flops 22018560 | bytes 23867392 | tf_op jit(solution)/shard_map/reduce_sum | solution.py:80
  105.5 11.2 %fusion.7 = bf16[128,3,512]{2,0,1:T(8,128)(2,1)S(1)} fusion(f32[3,512]{1,0:T(4,128)S(1)} %fusion, f32[3,512]{1,0:T(4,128)S(1)} %get-tuple-element.16, f32[3584,512,3]{1,0,2:T(8,128)} %copy-done, pred[512,3584]{0,1:T(8,128)(4,1)S(1)} %iota_compare_fusion, bf16[3584,1,2,128]{3,0,2,1:T(8,128)(2,1)} %maximum_maximum_fusion), kind=kOutput, calls=%fused_computation.17 | convolution fusion | flops 1437007872 | bytes 25178112 | tf_op jit(solution)/shard_map/kgsl,lkd->skgd/dot_general | solution.py:81
  116.7 4.7 %convolution_convert_fusion = bf16[512,5120]{1,0:T(8,128)(2,1)} fusion(bf16[512,384]{0,1:T(8,128)(2,1)S(1)} %bitcast.92, bf16[384,5120]{1,0:T(8,128)(2,1)S(1)} %copy-done.1), kind=kOutput, calls=%fused_computation.9 | convolution fusion | flops 2015887360 | bytes 9568256 | tf_op jit(solution)/shard_map/dot_general | solution.py:126
  124.7 15.4 %all_to_all.38 = f32[32,1,128]{2,1,0:T(1,128)S(1)} all-to-all(f32[32,1,128]{2,1,0:T(1,128)S(1)} %reshape.422), channel_id=1, replica_groups=mesh['branch'=32,'tensor'=8] {'branch'}, dimensions={0} | all-to-all | bytes 32768 | tf_op jit(solution)/shard_map/all_to_all | solution.py:15
  141.6 0.7 dynamic-slice_reduce_fusion
  142.4 20.1 %reduce-scatter.2.cloned.1.call-done = bf16[64,5120]{1,0:T(8,128)(2,1)} async-done(((bf16[512,5120]{1,0:T(8,128)(2,1)}), bf16[64,5120]{1,0:T(8,128)(2,1)}) %reduce-scatter.2.cloned.1.call-update) | async-done | bytes 655376 | tf_op jit(solution)/shard_map/reduce_scatter | solution.py:127
  (46 shorter events, 5.6 us)
Async XLA Ops:
  7.2 59.4 %all-gather.2.cloned.1.call-start = ((), (), s32[]{:S(2)}) async-start(), calls=%async_computation.4 | async-start | bytes 5898240 | tf_op jit(solution)/shard_map/all_gather | solution.py:104
  13.1 27.2 %all-to-all-start = ((bf16[1,2,512,256]{3,1,0,2:T(2,128)(2,1)}), bf16[1,2,512,256]{3,1,0,2:T(2,128)(2,1)S(1)}, u32[]{:S(2)}, u32[]{:S(2)}) async-start(bf16[1,2,512,256]{3,1,0,2:T(2,128)(2,1)} %bitcast.82), calls=%async_computation | async-start | bytes 1048576 | tf_op jit(solution)/shard_map/all_to_all | solution.py:116
  41.9 21.8 %all-to-all-start.1 = ((bf16[32,2,16,256]{3,2,1,0:T(8,128)(2,1)}), bf16[32,2,16,256]{3,2,1,0:T(8,128)(2,1)S(1)}, u32[]{:S(2)}, u32[]{:S(2)}) async-start(bf16[32,2,16,256]{3,2,1,0:T(8,128)(2,1)} %bitcast.10), calls=%async_computation.1 | async-start | bytes 1048576 | tf_op jit(solution)/shard_map/all_to_all | solution.py:120
  48.9 113.6 %reduce-scatter.2.cloned.1.call-start = ((), (), s32[]{:S(2)}) async-start(), calls=%async_computation.5 | async-start | bytes 5898240 | tf_op jit(solution)/shard_map/reduce_scatter | solution.py:127
  78.1 7.0 %copy-start.2 = (bf16[1024,1,2,128]{3,0,2,1:T(8,128)(2,1)S(1)}, bf16[1024,1,2,128]{3,0,2,1:T(8,128)(2,1)}, u32[]{:S(2)}) copy-start(bf16[1024,1,2,128]{3,0,2,1:T(8,128)(2,1)} %copy.77) | copy-start | bytes 1572868
  93.1 7.3 %copy-start = (f32[3584,512,3]{1,0,2:T(8,128)}, f32[3584,512,3]{1,0,2:T(8,128)S(1)}, u32[]{:S(2)}) copy-start(f32[3584,512,3]{1,0,2:T(8,128)S(1)} %get-tuple-element.17) | copy-start | bytes 66060292
  105.4 11.2 %copy-start.1 = (bf16[384,5120]{1,0:T(8,128)(2,1)S(1)}, bf16[384,5120]{1,0:T(8,128)(2,1)}, u32[]{:S(2)}) copy-start(bf16[384,5120]{1,0:T(8,128)(2,1)} %param.11) | copy-start | bytes 11796484
Sparse Core Ops, SparseCore 0:
  10.8 41.8 all-gather.1
  121.5 40.9 reduce-scatter.1
where the time goes:
time: 170 us; the launch traced here: 169 us
  waiting for transfers between devices  42.3 us (25%)
  matrix products  30 us (18%)
  local copies, waits for them, and re-layouts  26.2 us (15%)
  other arithmetic  21.5 us (13%)
  starting transfers between devices  19 us (11%)
  blocking collectives  15.4 us (9%)
  between operations  15 us (9%)
    reduce_scatter x1, waiting for transfers between devices, per_device(): lax.psum_scatter(partial_term.astype(jnp.bfloat16).astype(jnp.float32).as...  20.1 us
    unnamed x14, local copies, waits for them, and re-layouts  16.1 us
    all_to_all x1, blocking collectives, from_everyone(): lax.all_to_all(jnp.broadcast_to(x[None], (count, *x.shape)), axis, 0, 0,...  15.4 us
    all_to_all x1, waiting for transfers between devices, per_device(): lax.all_to_all(outgoing, 'branch', split_axis=0, concat_axis=2, tiled=True)  13 us
    all_to_all x1, starting transfers between devices, per_device(): lax.all_to_all(subtree_cache[None], 'branch', split_axis=2, concat_axis=0...  11.7 us
    dot_general x1, matrix products, attend(): jnp.einsum('kgsl,lkd->skgd', weights, values, preferred_element_type=jnp....  11.2 us
    all_to_all x1, waiting for transfers between devices, per_device(): lax.all_to_all(subtree_cache[None], 'branch', split_axis=2, concat_axis=0...  9.03 us
    dot_general x1, matrix products, per_device(): jnp.dot(lax.all_gather(normed, 'tensor', axis=0, tiled=True), projection_...  8.41 us
  transfers between devices with their start and end apart: 4, of which 3 were waited for; matrix products, arithmetic and copies ran while one was open for 11% of the time, Pallas kernels for 0%

commit v1 on v0

--- a/solution.py
+++ b/solution.py
@@ -113,7 +113,15 @@
     second = parents[1]
     first = parents[0][second]
     position = lax.axis_index("branch")
-    held = lax.all_to_all(subtree_cache[None], "branch", split_axis=2, concat_axis=0, tiled=True)
+    held = jnp.concatenate(
+        lax.all_to_all(
+            jnp.stack(jnp.split(subtree_cache[None], lax.axis_size("branch"), axis=2)),
+            "branch",
+            0,
+            0,
+        ),
+        axis=0,
+    )
     tree_levels = jnp.arange(2, dtype=jnp.int32)
     picks = jnp.stack([first, second], 1)
     outgoing = held[picks, tree_levels[None, :]]

time: 170 us -> 212 us (1.25); the launches traced: 169 us -> 209 us
  local copies, waits for them, and re-layouts: 26.2 us -> 65.9 us
    unnamed x14 -> x44, local copies, waits for them, and re-layouts: 16.1 us -> 54.5 us
  transfers between devices with their start and end apart: 4 -> 4, of which waited for: 3 -> 3; matrix products, arithmetic and copies ran while one was open for 11% -> 28% of each run, Pallas kernels for 0% -> 0%
where the time goes in v1:
time: 212 us; the launch traced here: 209 us
  local copies, waits for them, and re-layouts  65.9 us (31%)
  waiting for transfers between devices  42.3 us (20%)
  matrix products  30 us (14%)
  other arithmetic  21.5 us (10%)
  starting transfers between devices  19 us (9%)
  blocking collectives  15.4 us (7%)
  between operations  15 us (7%)
    unnamed x44, local copies, waits for them, and re-layouts  54.5 us
    reduce_scatter x1, waiting for transfers between devices, per_device(): lax.psum_scatter(partial_term.astype(jnp.bfloat16).astype(jnp.float32).as...  20.2 us
    all_to_all x1, blocking collectives, from_everyone(): lax.all_to_all(jnp.broadcast_to(x[None], (count, *x.shape)), axis, 0, 0,...  15.4 us
    all_to_all x1, waiting for transfers between devices, per_device(): lax.all_to_all(outgoing, 'branch', split_axis=0, concat_axis=2, tiled=True)  13.1 us
    all_to_all x1, starting transfers between devices, per_device(): lax.all_to_all(jnp.stack(jnp.split(subtree_cache[None], lax.axis_size('br...  11.8 us
    dot_general x1, matrix products, attend(): jnp.einsum('kgsl,lkd->skgd', weights, values, preferred_element_type=jnp....  11.2 us
    all_to_all x1, waiting for transfers between devices, per_device(): lax.all_to_all(jnp.stack(jnp.split(subtree_cache[None], lax.axis_size('br...  9.07 us
    dot_general x1, matrix products, per_device(): jnp.dot(lax.all_gather(normed, 'tensor', axis=0, tiled=True), projection_...  8.41 us
  transfers between devices with their start and end apart: 4, of which 3 were waited for; matrix products, arithmetic and copies ran while one was open for 28% of the time, Pallas kernels for 0%

profile of v1, /device:TPU:8, one launch (start us, length us, event | category | flops | bytes accessed | tf_op | source)
XLA Modules:
  0.0 209.1 jit_solution(2922210674990851406)
XLA Ops:
  8.5 2.2 %fusion.6 = bf16[64,5120]{1,0:T(8,128)(2,1)} fusion(bf16[64,5120]{1,0:T(8,128)(2,1)} %param.8, f32[5120]{0:T(1024)} %param.9, f32[64]{0:T(128)S(1)} %add_rsqrt_fusion), kind=kLoop, calls=%fused_computation.16 | loop fusion | flops 1310720 | bytes 1331456 | tf_op jit(solution)/shard_map/convert_element_type | solution.py:51
  12.0 1.3 constant_dynamic-update-slice_fusion.30
  13.4 1.3 constant_dynamic-update-slice_fusion.29
  18.6 1.3 constant_dynamic-update-slice_fusion.25
  31.8 1.3 constant_dynamic-update-slice_fusion.15
  33.1 1.3 constant_dynamic-update-slice_fusion.14
  34.4 1.3 constant_dynamic-update-slice_fusion.13
  39.7 1.3 constant_dynamic-update-slice_fusion.9
  41.0 1.3 constant_dynamic-update-slice_fusion.8
  47.6 1.3 constant_dynamic-update-slice_fusion.3
  50.3 1.3 constant_dynamic-update-slice_fusion.1
  52.9 11.8 %all-to-all-start = ((bf16[32,1,2,16,256]{4,3,2,1,0:T(8,128)(2,1)}), bf16[32,1,2,16,256]{4,3,2,1,0:T(8,128)(2,1)S(1)}, u32[]{:S(2)}, u32[]{:S(2)}) async-start(bf16[32,1,2,16,256]{4,3,2,1,0:T(8,128)(2,1)} %constant_dynamic-update-slice_fusion), calls=%async_computation | async-start | bytes 1048576 | tf_op jit(solution)/shard_map/all_to_all | solution.py:117
  67.0 1.5 copy.42
  69.2 1.8 multiply_cosine_fusion
  71.1 9.1 %all-to-all-done = bf16[32,1,2,16,256]{4,3,2,1,0:T(8,128)(2,1)S(1)} async-done(((bf16[32,1,2,16,256]{4,3,2,1,0:T(8,128)(2,1)}), bf16[32,1,2,16,256]{4,3,2,1,0:T(8,128)(2,1)S(1)}, u32[]{:S(2)}, u32[]{:S(2)}) %all-to-all-start) | async-done | bytes 524320 | tf_op jit(solution)/shard_map/all_to_all | solution.py:117
  80.1 1.5 gather_fusion.1
  81.6 7.0 %all-to-all-start.1 = ((bf16[32,2,16,256]{3,2,1,0:T(8,128)(2,1)}), bf16[32,2,16,256]{3,2,1,0:T(8,128)(2,1)S(1)}, u32[]{:S(2)}, u32[]{:S(2)}) async-start(bf16[32,2,16,256]{3,2,1,0:T(8,128)(2,1)} %bitcast.40), calls=%async_computation.1 | async-start | bytes 1048576 | tf_op jit(solution)/shard_map/all_to_all | solution.py:128
  88.9 1.5 iota_compare_fusion
  90.4 13.1 %all-to-all-done.1 = bf16[32,2,16,256]{3,2,1,0:T(8,128)(2,1)S(1)} async-done(((bf16[32,2,16,256]{3,2,1,0:T(8,128)(2,1)}), bf16[32,2,16,256]{3,2,1,0:T(8,128)(2,1)S(1)}, u32[]{:S(2)}, u32[]{:S(2)}) %all-to-all-start.1) | async-done | bytes 524320 | tf_op jit(solution)/shard_map/all_to_all | solution.py:128
  106.3 8.4 %fusion.37 = f32[512,640]{0,1:T(8,128)S(1)} fusion(bf16[512,5120]{1,0:T(8,128)(2,1)} %all-gather.2.cloned.1.call-done, bf16[5120,640]{1,0:T(8,128)(2,1)} %param.10), kind=kOutput, calls=%fused_computation.142 | convolution fusion | flops 3355443200 | bytes 13107200 | tf_op jit(solution)/shard_map/dot_general | solution.py:103
  116.0 1.9 fusion.25
  117.8 2.2 %copy.61 = f32[512,1,3,64]{3,0,2,1:T(8,128)} copy(f32[512,1,3,64]{0,3,2,1:T(8,128)} %get-tuple-element.5) | data formatting | bytes 786432
  120.0 2.2 %copy.60 = f32[512,1,3,64]{3,0,2,1:T(8,128)} copy(f32[512,1,3,64]{0,3,2,1:T(8,128)} %get-tuple-element.6) | data formatting | bytes 786432
  122.2 2.6 %fusion.11 = (bf16[512,3,64]{2,0,1:T(8,128)(2,1)}, bf16[512,3,64]{2,0,1:T(8,128)(2,1)}) fusion(f32[512,1,3,64]{3,0,2,1:T(8,128)} %copy.61, f32[512,1,3,64]{3,0,2,1:T(8,128)} %copy.60, f32[512,64]{1,0:T(8,128)} %get-tuple-element.12, f32[512,64]{1,0:T(8,128)} %get-tuple-element.11), kind=kLoop, calls=%fused_computation.23 | loop fusion | flops 786432 | bytes 1441792 | tf_op jit(solution)/shard_map/concatenate | solution.py:64
  124.8 2.4 %maximum_maximum_fusion = bf16[3584,1,2,128]{3,0,2,1:T(8,128)(2,1)} fusion(bf16[512,1,1,128]{3,0,2,1:T(8,128)(2,1)S(1)} %copy.59, bf16[512,1,1,64]{3,0,2,1:T(8,128)(2,1)} %get-tuple-element.8, bf16[512,1,1,64]{3,0,2,1:T(8,128)(2,1)} %get-tuple-element.7, bf16[1024,1,2,128]{3,0,2,1:T(8,128)(2,1)S(1)} %copy-done.2, bf16[2048,1,2,128]{3,0,2,1:T(8,128)(2,1)S(1)} %copy.48), kind=kLoop, calls=%fused_computation.11 | loop fusion | flops 9175040 | bytes 3670016 | tf_op jit(solution)/shard_map/concatenate | solution.py:132
  127.2 5.6 %fusion.1 = (f32[3,512]{1,0:T(4,128)S(1)}, f32[3584,512,3]{1,0,2:T(8,128)S(1)}) fusion(pred[512,3584]{0,1:T(8,128)(4,1)S(1)} %iota_compare_fusion, bf16[512,3,64]{2,0,1:T(8,128)(2,1)} %get-tuple-element.4, bf16[512,3,64]{2,0,1:T(8,128)(2,1)} %get-tuple-element.3, bf16[3584,1,2,128]{3,0,2,1:T(8,128)(2,1)} %maximum_maximum_fusion), kind=kOutput, calls=%fused_computation.6 | convolution fusion | flops 1426586112 | bytes 25565184 | tf_op jit(solution)/shard_map/skgd,lkd->kgsl/dot_general | solution.py:71
  132.9 7.3 %copy-done = f32[3584,512,3]{1,0,2:T(8,128)} copy-done((f32[3584,512,3]{1,0,2:T(8,128)}, f32[3584,512,3]{1,0,2:T(8,128)S(1)}, u32[]{:S(2)}) %copy-start) | copy-done | bytes 22020120
  140.2 5.0 %fusion = f32[3,512]{1,0:T(4,128)S(1)} fusion(f32[3584,512,3]{1,0,2:T(8,128)S(1)} %get-tuple-element.17, f32[3,512]{1,0:T(4,128)S(1)} %get-tuple-element.16, pred[512,3584]{0,1:T(8,128)(4,1)S(1)} %iota_compare_fusion), kind=kLoop, calls=%fused_computation.5 | loop fusion | flops 22018560 | bytes 23867392 | tf_op jit(solution)/shard_map/reduce_sum | solution.py:80
  145.2 11.2 %fusion.7 = bf16[128,3,512]{2,0,1:T(8,128)(2,1)S(1)} fusion(f32[3,512]{1,0:T(4,128)S(1)} %fusion, f32[3,512]{1,0:T(4,128)S(1)} %get-tuple-element.16, f32[3584,512,3]{1,0,2:T(8,128)} %copy-done, pred[512,3584]{0,1:T(8,128)(4,1)S(1)} %iota_compare_fusion, bf16[3584,1,2,128]{3,0,2,1:T(8,128)(2,1)} %maximum_maximum_fusion), kind=kOutput, calls=%fused_computation.17 | convolution fusion | flops 1437007872 | bytes 25178112 | tf_op jit(solution)/shard_map/kgsl,lkd->skgd/dot_general | solution.py:81
  156.4 4.7 %convolution_convert_fusion = bf16[512,5120]{1,0:T(8,128)(2,1)} fusion(bf16[512,384]{0,1:T(8,128)(2,1)S(1)} %bitcast.244, bf16[384,5120]{1,0:T(8,128)(2,1)S(1)} %copy-done.1), kind=kOutput, calls=%fused_computation.9 | convolution fusion | flops 2015887360 | bytes 9568256 | tf_op jit(solution)/shard_map/dot_general | solution.py:134
  164.5 15.4 %all_to_all.25 = f32[32,1,128]{2,1,0:T(1,128)S(1)} all-to-all(f32[32,1,128]{2,1,0:T(1,128)S(1)} %reshape.426), channel_id=1, replica_groups=mesh['branch'=32,'tensor'=8] {'branch'}, dimensions={0} | all-to-all | bytes 32768 | tf_op jit(solution)/shard_map/all_to_all | solution.py:15
  182.1 20.2 %reduce-scatter.2.cloned.1.call-done = bf16[64,5120]{1,0:T(8,128)(2,1)} async-done(((bf16[512,5120]{1,0:T(8,128)(2,1)}), bf16[64,5120]{1,0:T(8,128)(2,1)}) %reduce-scatter.2.cloned.1.call-update) | async-done | bytes 655376 | tf_op jit(solution)/shard_map/reduce_scatter | solution.py:135
  (76 shorter events, 42.4 us)
Async XLA Ops:
  7.2 99.1 %all-gather.2.cloned.1.call-start = ((), (), s32[]{:S(2)}) async-start(), calls=%async_computation.4 | async-start | bytes 5898240 | tf_op jit(solution)/shard_map/all_gather | solution.py:104
  52.9 27.2 %all-to-all-start = ((bf16[32,1,2,16,256]{4,3,2,1,0:T(8,128)(2,1)}), bf16[32,1,2,16,256]{4,3,2,1,0:T(8,128)(2,1)S(1)}, u32[]{:S(2)}, u32[]{:S(2)}) async-start(bf16[32,1,2,16,256]{4,3,2,1,0:T(8,128)(2,1)} %constant_dynamic-update-slice_fusion), calls=%async_computation | async-start | bytes 1048576 | tf_op jit(solution)/shard_map/all_to_all | solution.py:117
  81.6 21.8 %all-to-all-start.1 = ((bf16[32,2,16,256]{3,2,1,0:T(8,128)(2,1)}), bf16[32,2,16,256]{3,2,1,0:T(8,128)(2,1)S(1)}, u32[]{:S(2)}, u32[]{:S(2)}) async-start(bf16[32,2,16,256]{3,2,1,0:T(8,128)(2,1)} %bitcast.40), calls=%async_computation.1 | async-start | bytes 1048576 | tf_op jit(solution)/shard_map/all_to_all | solution.py:128
  88.6 113.7 %reduce-scatter.2.cloned.1.call-start = ((), (), s32[]{:S(2)}) async-start(), calls=%async_computation.5 | async-start | bytes 5898240 | tf_op jit(solution)/shard_map/reduce_scatter | solution.py:135
  117.8 7.0 %copy-start.2 = (bf16[1024,1,2,128]{3,0,2,1:T(8,128)(2,1)S(1)}, bf16[1024,1,2,128]{3,0,2,1:T(8,128)(2,1)}, u32[]{:S(2)}) copy-start(bf16[1024,1,2,128]{3,0,2,1:T(8,128)(2,1)} %copy.49) | copy-start | bytes 1572868
  132.8 7.3 %copy-start = (f32[3584,512,3]{1,0,2:T(8,128)}, f32[3584,512,3]{1,0,2:T(8,128)S(1)}, u32[]{:S(2)}) copy-start(f32[3584,512,3]{1,0,2:T(8,128)S(1)} %get-tuple-element.17) | copy-start | bytes 66060292
  145.2 11.2 %copy-start.1 = (bf16[384,5120]{1,0:T(8,128)(2,1)S(1)}, bf16[384,5120]{1,0:T(8,128)(2,1)}, u32[]{:S(2)}) copy-start(bf16[384,5120]{1,0:T(8,128)(2,1)} %param.11) | copy-start | bytes 11796484
Sparse Core Ops, SparseCore 0:
  10.8 41.8 all-gather.1
  161.3 40.9 reduce-scatter.1
